TPU v7x, 16 devices: a 4x2x1 block of a 4x4x8 slice. The times are simulated.
16 devices in a mesh: dp: 2 (over y, z), tp: 8 (over x, core).
Axes of the slice: x: 4, y: 2, z: 1, core: 2. Of those that a mesh axis runs over, the one named last changes fastest.
The devices are a block of a 4x4x8 slice.
Arguments:
- token_act: bfloat16 [16, 1536, 768], P('dp'), parts along dimension 0
- token_cond: bfloat16 [16, 1536, 384], P('dp'), parts along dimension 0
- pair_bias: bfloat16 [2, 16, 1536, 1536], P(None, 'tp')
- token_mask: int32 [1536], replicated
- ada_scale: float32 [2, 2, 384], replicated
- ada_w: bfloat16 [2, 2, 384, 2, 768], replicated
- ada_bias: float32 [2, 2, 768], replicated
- zero_w: bfloat16 [2, 384, 2, 768], replicated
- zero_b: float32 [2, 2, 768], replicated
- w_qkvg: bfloat16 [2, 768, 4, 768], P(None, None, None, 'tp')
- b_q: float32 [2, 768], P(None, 'tp')
- w_o: bfloat16 [2, 768, 768], P(None, 'tp')
- w_up: bfloat16 [2, 768, 2, 1536], P(None, None, None, 'tp')
- w_down: bfloat16 [2, 1536, 768], P(None, 'tp')
Outputs:
- output: bfloat16 [16, 1536, 768], P('dp'), parts along dimension 0
There are 2 independent parts. A program takes and returns all parts, laid end to end along the dimension named above; an argument that names none is the same for every part.
All inputs are finite; a program needn't handle non-finite values.
Results may differ from a plain program's by a relative error of at most 0.0179886.
Values are sent between devices in bfloat16 or wider.
A program may use at most 768 MiB of HBM per device.

v0:
```python
import math
import functools
import jax
import jax.numpy as jnp
from jax import lax
from jax.sharding import PartitionSpec as P

LN_EPS = 1e-5


def layer_norm(values_in):
    row_mean = jnp.mean(values_in, axis=-1, keepdims=True)
    centered = values_in - row_mean
    variance = jnp.mean(centered * centered, axis=-1, keepdims=True)
    return centered * lax.rsqrt(variance + LN_EPS)


def ada_norm(act_f32, cond_normed, scale_vec, weight, bias_vec):
    cond_in = (cond_normed * scale_vec).astype(jnp.bfloat16)
    modulation = jnp.einsum('rc,cgd->rgd', cond_in, weight, preferred_element_type=jnp.float32)
    return (jax.nn.sigmoid(modulation[:, 0] + bias_vec) * layer_norm(act_f32) + modulation[:, 1]).astype(jnp.bfloat16)


def attend_sample(bias_layer, mask_add, logit_scale, operands):
    query_one, key_one, value_one = operands
    logits = jnp.einsum('qhc,khc->hqk', query_one, key_one, preferred_element_type=jnp.float32) * logit_scale + bias_layer + mask_add
    attn_probs = jax.nn.softmax(logits, axis=-1).astype(jnp.bfloat16)
    return jnp.einsum('hqk,khc->qhc', attn_probs, value_one, preferred_element_type=jnp.float32)


def solution(mesh):
    def shard_body(token_act, token_cond, pair_bias, token_mask, ada_scale, ada_w, ada_bias, zero_w, zero_b, w_qkvg, b_q, w_o, w_up, w_down):
        samples, tokens, model_width = token_act.shape
        cond_dim = token_cond.shape[-1]
        heads_local = pair_bias.shape[1]
        local_width = w_qkvg.shape[-1]
        head_dim = local_width // heads_local
        row_count = samples * tokens
        head_shape = (samples, tokens, heads_local, head_dim)
        logit_scale = 1.0 / math.sqrt(head_dim)
        mask_add = (token_mask.astype(jnp.float32) - 1.0) * 1e9
        cond_flat = token_cond.reshape(row_count, cond_dim)
        cond_normed = layer_norm(cond_flat.astype(jnp.float32))
        act_flat = token_act.reshape(row_count, model_width)
        for layer_idx in range(pair_bias.shape[0]):
            out_gates = jax.nn.sigmoid(jnp.einsum('rc,cgd->rgd', cond_flat, zero_w[layer_idx], preferred_element_type=jnp.float32) + zero_b[layer_idx])
            act_f32 = act_flat.astype(jnp.float32)
            normed = ada_norm(act_f32, cond_normed, ada_scale[layer_idx, 0], ada_w[layer_idx, 0], ada_bias[layer_idx, 0])
            projected = jnp.einsum('rd,dfe->rfe', normed, w_qkvg[layer_idx], preferred_element_type=jnp.float32)
            query_rows = (projected[:, 0] + b_q[layer_idx]).astype(jnp.bfloat16).reshape(head_shape)
            key_rows = projected[:, 1].astype(jnp.bfloat16).reshape(head_shape)
            value_rows = projected[:, 2].astype(jnp.bfloat16).reshape(head_shape)
            gate_heads = jax.nn.sigmoid(projected[:, 3])
            attend_layer = functools.partial(attend_sample, pair_bias[layer_idx], mask_add, logit_scale)
            mixed_heads = lax.map(attend_layer, (query_rows, key_rows, value_rows)).reshape(row_count, local_width)
            heads_out = (gate_heads * mixed_heads).astype(jnp.bfloat16)
            attn_part = jnp.dot(heads_out, w_o[layer_idx], preferred_element_type=jnp.float32).astype(jnp.bfloat16)
            attn_out = lax.psum(attn_part, 'tp').astype(jnp.float32)
            mid_f32 = (act_f32 + out_gates[:, 0] * attn_out).astype(jnp.bfloat16).astype(jnp.float32)
            normed_mid = ada_norm(mid_f32, cond_normed, ada_scale[layer_idx, 1], ada_w[layer_idx, 1], ada_bias[layer_idx, 1])
            hidden_pre = jnp.einsum('rd,dgf->rgf', normed_mid, w_up[layer_idx], preferred_element_type=jnp.float32)
            hidden = (jax.nn.silu(hidden_pre[:, 0]) * hidden_pre[:, 1]).astype(jnp.bfloat16)
            trans_part = jnp.dot(hidden, w_down[layer_idx], preferred_element_type=jnp.float32).astype(jnp.bfloat16)
            trans_out = lax.psum(trans_part, 'tp').astype(jnp.float32)
            act_flat = (mid_f32 + out_gates[:, 1] * trans_out).astype(jnp.bfloat16)
        return act_flat.reshape(samples, tokens, model_width)

    everywhere = P()
    in_specs = (P('dp', None, None), P('dp', None, None), P(None, 'tp', None, None), P(None), everywhere, everywhere, everywhere, everywhere, everywhere, P(None, None, None, 'tp'), P(None, 'tp'), P(None, 'tp', None), P(None, None, None, 'tp'), P(None, 'tp', None))
    return jax.shard_map(shard_body, mesh=mesh, in_specs=in_specs, out_specs=P('dp', None, None), check_vma=False)
```

profile of v0, /device:TPU:113, one launch (start us, length us, event | category | flops | bytes accessed | tf_op | source)
XLA Modules:
  0.0 1772.4 jit_solution(18035168844570474693)
XLA Ops:
  44.7 22.4 %fusion.144 = (bf16[8,1536,384]{2,1,0:T(8,128)(2,1)}, bf16[8,1536,384]{2,1,0:T(8,128)(2,1)}, bf16[8,1536,384]{2,1,0:T(8,128)(2,1)}, bf16[8,1536,384]{2,1,0:T(8,128)(2,1)}) fusion(bf16[8,1536,384]{2,1,0:T(8,128)(2,1)} %param.19, f32[384]{0:T(512)S(1)} %get-tuple-element.113, f32[8,1536]{1,0:T(8,128)} %add_rsqrt_fusion.4, ...), kind=kLoop, calls=%fused_computation.145 | loop fusion | flops 51904512 | bytes 47290368 | tf_op jit(solution)/shard_map/convert_element_type | solution.py:19
  67.1 34.8 %fusion.173 = f32[12288,2,768]{2,0,1:T(8,128)} fusion(bf16[12288,384,1]{1,0,2:T(8,128)(2,1)} %bitcast.344, bf16[1,1,384,2,768]{4,3,2,1,0:T(2,128)(2,1)S(1)} %get-tuple-element.170), kind=kOutput, calls=%fused_computation.183 | convolution fusion | flops 14495514624 | bytes 86114304 | tf_op jit(solution)/shard_map/rc,cgd->rgd/dot_general | solution.py:20
  101.9 37.2 %fusion.125 = bf16[12288,1,768]{2,0,1:T(8,128)(2,1)} fusion(f32[12288,2,768]{2,0,1:T(8,128)} %fusion.173, bf16[8,1536,768]{2,1,0:T(8,128)(2,1)} %param.18, f32[12288]{0:T(1024)S(1)} %rsqrt.45, f32[12288]{0:T(1024)S(1)} %copy-done.16, f32[768]{0:T(1024)S(1)} %get-tuple-element.111), kind=kLoop, calls=%fused_computation.116 | loop fusion | flops 94371840 | bytes 113347584 | tf_op jit(solution)/shard_map/convert_element_type | solution.py:21
  139.1 27.2 %fusion.146 = f32[12288,384]{0,1} fusion(bf16[768,384]{0,1:T(8,128)(2,1)S(1)} %bitcast.378, bf16[12288,1,768]{2,0,1:T(8,128)(2,1)} %fusion.125), kind=kOutput, calls=%fused_computation.147 | convolution fusion | flops 7247757312 | bytes 38338560
  233.0 179.2 %while.20 = (s32[]{:T(128)}, f32[8,1536,2,48]{1,3,2,0:T(8,128)}, bf16[8,1536,2,48]{1,3,2,0:T(8,128)(2,1)S(1)}, bf16[8,1536,2,48]{1,3,2,0:T(8,128)(2,1)}, bf16[8,...) while((s32[]{:T(128)}, f32[8,1536,2,48]{1,3,2,0:T(8,128)}, ...), condition=%wide.region_7.8_spmd, body=%wide.region_4.7_spmd.sunk | while | flops 1420302336 | bytes 20980820 | solution.py:55
  441.1 34.3 %fusion.172 = f32[12288,2,768]{2,0,1:T(8,128)} fusion(bf16[12288,384,1]{1,0,2:T(8,128)(2,1)} %bitcast.343, bf16[1,1,384,2,768]{4,3,2,1,0:T(2,128)(2,1)S(1)} %copy-done.6), kind=kOutput, calls=%fused_computation.181 | convolution fusion | flops 14495514624 | bytes 86114304 | tf_op jit(solution)/shard_map/rc,cgd->rgd/dot_general | solution.py:20
  475.4 43.3 %add_divide_fusion.1 = f32[12288,2,768]{2,0,1:T(8,128)} fusion(f32[2,768]{1,0:T(2,128)S(1)} %get-tuple-element.178, bf16[12288,384,1]{1,0,2:T(8,128)(2,1)} %bitcast.339, bf16[1,384,2,768]{3,2,1,0:T(2,128)(2,1)S(1)} %copy-done.10), kind=kOutput, calls=%fused_computation.57 | convolution fusion | flops 14571012096 | bytes 86120448 | tf_op jit(solution)/shard_map/rc,cgd->rgd/dot_general | solution.py:46
  518.7 113.1 %all-reduce.5.cloned.1.call-done = bf16[12288,768]{1,0:T(8,128)(2,1)} async-done(((bf16[12288,768]{1,0:T(8,128)(2,1)}), bf16[12288,768]{1,0:T(8,128)(2,1)}) %all-reduce.5.cloned.1.call-update) | async-done | bytes 18874384 | tf_op jit(solution)/shard_map/psum | solution.py:58
  631.8 31.3 %convert_reduce_fusion.2 = (f32[12288]{0:T(1024)S(1)}, bf16[12288,768]{1,0:T(8,128)(2,1)}) fusion(bf16[12288,768]{1,0:T(8,128)(2,1)} %all-reduce.5.cloned.1.call-done, f32[12288,2,768]{2,0,1:T(8,128)} %add_divide_fusion.1, bf16[8,1536,768]{2,1,0:T(8,128)(2,1)} %param.18), kind=kLoop, calls=%fused_computation.66 | loop fusion | flops 66048000 | bytes 94420992 | tf_op jit(solution)/shard_map/reduce_sum | solution.py:12
  677.4 38.4 %fusion.148 = f32[12288,384]{0,1} fusion(bf16[768,384]{0,1:T(8,128)(2,1)S(1)} %bitcast.377, bf16[12288,768]{1,0:T(8,128)(2,1)} %get-tuple-element.152, f32[12288,2,768]{2,0,1:T(8,128)} %fusion.172, f32[12288]{0:T(1024)S(1)} %add_rsqrt_fusion.2, f32[12288]{0:T(1024)S(1)} %broadcast_multiply_fusion.2, f32[768]{0:T(1024)S(1)} %copy-done.26), kind=kOutput, calls=%fused_computation.150 | convolution fusion | flops 7342129152 | bytes 113937408
  715.7 14.7 convolution_convert_fusion.2
  744.4 34.1 %fusion.171 = f32[12288,2,768]{2,0,1:T(8,128)} fusion(bf16[12288,384,1]{1,0,2:T(8,128)(2,1)} %bitcast.342, bf16[1,1,384,2,768]{4,3,2,1,0:T(2,128)(2,1)S(1)} %copy-done.5), kind=kOutput, calls=%fused_computation.178 | convolution fusion | flops 14495514624 | bytes 86114304 | tf_op jit(solution)/shard_map/rc,cgd->rgd/dot_general | solution.py:20
  778.5 34.3 %fusion.170 = f32[12288,2,768]{2,0,1:T(8,128)} fusion(bf16[12288,384,1]{1,0,2:T(8,128)(2,1)} %bitcast.341, bf16[1,1,384,2,768]{4,3,2,1,0:T(2,128)(2,1)S(1)} %copy-done.4), kind=kOutput, calls=%fused_computation.176 | convolution fusion | flops 14495514624 | bytes 86114304 | tf_op jit(solution)/shard_map/rc,cgd->rgd/dot_general | solution.py:20
  812.8 111.9 %all-reduce.7.cloned.1.call-done = bf16[12288,768]{1,0:T(8,128)(2,1)} async-done(((bf16[12288,768]{1,0:T(8,128)(2,1)}), bf16[12288,768]{1,0:T(8,128)(2,1)}) %all-reduce.7.cloned.1.call-update) | async-done | bytes 18874384 | tf_op jit(solution)/shard_map/psum | solution.py:64
  924.7 31.4 %convert_reduce_fusion.1 = (f32[12288]{0:T(1024)S(1)}, bf16[12288,768]{1,0:T(8,128)(2,1)}) fusion(bf16[12288,768]{1,0:T(8,128)(2,1)} %all-reduce.7.cloned.1.call-done, f32[12288,2,768]{2,0,1:T(8,128)} %add_divide_fusion.1, bf16[12288,768]{1,0:T(8,128)(2,1)} %get-tuple-element.152), kind=kLoop, calls=%fused_computation.63 | loop fusion | flops 66048000 | bytes 94420992 | tf_op jit(solution)/shard_map/reduce_sum | solution.py:12
  970.3 38.0 %fusion.150 = f32[12288,384]{0,1} fusion(bf16[768,384]{0,1:T(8,128)(2,1)S(1)} %bitcast.375, bf16[12288,768]{1,0:T(8,128)(2,1)} %get-tuple-element.150, f32[12288,2,768]{2,0,1:T(8,128)} %fusion.171, f32[12288]{0:T(1024)S(1)} %add_rsqrt_fusion.1, f32[12288]{0:T(1024)S(1)} %broadcast_multiply_fusion.1, f32[768]{0:T(1024)S(1)} %copy-done.25), kind=kOutput, calls=%fused_computation.151 | convolution fusion | flops 7342129152 | bytes 113937408
  1045.8 179.3 %while.21 = (s32[]{:T(128)}, f32[8,1536,2,48]{1,3,2,0:T(8,128)}, bf16[8,1536,2,48]{1,3,2,0:T(8,128)(2,1)S(1)}, bf16[8,1536,2,48]{1,3,2,0:T(8,128)(2,1)}, bf16[8,...) while((s32[]{:T(128)}, f32[8,1536,2,48]{1,3,2,0:T(8,128)}, ...), condition=%wide.region_17.18_spmd, body=%wide.region_14.17_spmd.sunk | while | flops 1420302336 | bytes 20980820 | solution.py:55
  1247.3 43.4 %add_divide_fusion = f32[12288,2,768]{2,0,1:T(8,128)} fusion(f32[2,768]{1,0:T(2,128)S(1)} %copy-done.23, bf16[12288,384,1]{1,0,2:T(8,128)(2,1)} %bitcast.340, bf16[1,384,2,768]{3,2,1,0:T(2,128)(2,1)S(1)} %copy-done.9), kind=kOutput, calls=%fused_computation.56 | convolution fusion | flops 14571012096 | bytes 86120448 | tf_op jit(solution)/shard_map/rc,cgd->rgd/dot_general | solution.py:46
  1290.7 150.6 %all-reduce.9.cloned.1.call-done = bf16[12288,768]{1,0:T(8,128)(2,1)} async-done(((bf16[12288,768]{1,0:T(8,128)(2,1)}), bf16[12288,768]{1,0:T(8,128)(2,1)}) %all-reduce.9.cloned.1.call-update) | async-done | bytes 18874384 | tf_op jit(solution)/shard_map/psum | solution.py:58
  1441.3 31.4 %convert_reduce_fusion = (f32[12288]{0:T(1024)S(1)}, bf16[12288,768]{1,0:T(8,128)(2,1)}) fusion(bf16[12288,768]{1,0:T(8,128)(2,1)} %all-reduce.9.cloned.1.call-done, f32[12288,2,768]{2,0,1:T(8,128)} %add_divide_fusion, bf16[12288,768]{1,0:T(8,128)(2,1)} %get-tuple-element.150), kind=kLoop, calls=%fused_computation.60 | loop fusion | flops 66048000 | bytes 94420992 | tf_op jit(solution)/shard_map/reduce_sum | solution.py:12
  1487.0 38.3 %fusion.152 = f32[12288,384]{0,1} fusion(bf16[768,384]{0,1:T(8,128)(2,1)S(1)} %bitcast.376, bf16[12288,768]{1,0:T(8,128)(2,1)} %get-tuple-element.148, f32[12288,2,768]{2,0,1:T(8,128)} %fusion.170, f32[12288]{0:T(1024)S(1)} %add_rsqrt_fusion, f32[12288]{0:T(1024)S(1)} %broadcast_multiply_fusion, f32[768]{0:T(1024)S(1)} %copy-done.24), kind=kOutput, calls=%fused_computation.152 | convolution fusion | flops 7342129152 | bytes 113937408
  1525.3 14.7 convolution_convert_fusion
  1540.1 194.1 %all-reduce.11.cloned.1.call-done = bf16[12288,768]{1,0:T(8,128)(2,1)} async-done(((bf16[12288,768]{1,0:T(8,128)(2,1)}), bf16[12288,768]{1,0:T(8,128)(2,1)}) %all-reduce.11.cloned.1.call-update) | async-done | bytes 18874384 | tf_op jit(solution)/shard_map/psum | solution.py:64
  1734.3 31.2 %fusion.106 = bf16[12288,768]{1,0:T(8,128)(2,1)} fusion(bf16[12288,768]{1,0:T(8,128)(2,1)} %get-tuple-element.148, f32[12288,2,768]{2,0,1:T(8,128)} %add_divide_fusion, bf16[12288,768]{1,0:T(8,128)(2,1)} %all-reduce.11.cloned.1.call-done), kind=kLoop, calls=%fused_computation.87 | loop fusion | flops 47185920 | bytes 94371840 | tf_op jit(solution)/shard_map/convert_element_type | solution.py:65
  (177 shorter events, 607.1 us)
Async XLA Ops:
  6.5 19.5 %copy-start.22 = (f32[2,2,384]{2,1,0:T(2,128)S(1)}, f32[2,2,384]{2,1,0:T(2,128)}, u32[]{:S(2)}) copy-start(f32[2,2,384]{2,1,0:T(2,128)} %param.22) | copy-start | bytes 18436
  6.5 625.2 %all-reduce.5.cloned.1.call-start = ((), (), s32[]{:S(2)}) async-start(), calls=%async_computation | async-start | bytes 37748736 | tf_op jit(solution)/shard_map/psum | solution.py:58
  18.6 20.3 %slice-start.2 = ((s8[4718592]{0:T(1024)(128)(4,1)}), s8[524288]{0:T(1024)(128)(4,1)S(1)}, s32[]{:S(2)}) async-start(s8[4718592]{0:T(1024)(128)(4,1)} %bitcast.373), calls=%async_computation.6 | async-start | bytes 1048576
  25.4 17.7 copy-start.17
  25.4 18.3 %copy-start.8 = (bf16[2,768,4,96]{1,3,2,0:T(8,128)(2,1)S(1)}, bf16[2,768,4,96]{1,3,2,0:T(8,128)(2,1)}, u32[]{:S(2)}) copy-start(bf16[2,768,4,96]{1,3,2,0:T(8,128)(2,1)} %param.27) | copy-start | bytes 3538948
  67.1 34.8 %copy-start.16 = (f32[12288]{0:T(1024)S(1)}, f32[12288]{0:T(1024)}, u32[]{:S(2)}) copy-start(f32[12288]{0:T(1024)} %div.95) | copy-start | bytes 147460
  412.2 13.0 copy-start.20
  412.2 13.0 copy-start.14
  434.8 489.9 %all-reduce.7.cloned.1.call-start = ((), (), s32[]{:S(2)}) async-start(), calls=%async_computation.1 | async-start | bytes 37748736 | tf_op jit(solution)/shard_map/psum | solution.py:64
  441.1 34.3 %copy-start.10 = (bf16[1,384,2,768]{3,2,1,0:T(2,128)(2,1)S(1)}, bf16[1,384,2,768]{3,2,1,0:T(2,128)(2,1)}, u32[]{:S(2)}) copy-start(bf16[1,384,2,768]{3,2,1,0:T(2,128)(2,1)} %get-tuple-element.172) | copy-start | bytes 3538948
  663.1 14.3 copy-start.13
  663.1 14.3 copy-start.26
  677.4 38.4 %copy-start.30 = (bf16[2,192,768]{2,1,0:T(8,128)(2,1)S(1)}, bf16[2,192,768]{2,1,0:T(8,128)(2,1)}, u32[]{:S(2)}) copy-start(bf16[2,192,768]{2,1,0:T(8,128)(2,1)} %param.31) | copy-start | bytes 1769476
  730.5 13.9 copy-start.5
  730.5 710.8 %all-reduce.9.cloned.1.call-start = ((), (), s32[]{:S(2)}) async-start(), calls=%async_computation.2 | async-start | bytes 37748736 | tf_op jit(solution)/shard_map/psum | solution.py:58
  744.4 34.1 %copy-start.4 = (bf16[1,1,384,2,768]{4,3,2,1,0:T(2,128)(2,1)S(1)}, bf16[1,1,384,2,768]{4,3,2,1,0:T(2,128)(2,1)}, u32[]{:S(2)}) copy-start(bf16[1,1,384,2,768]{4,3,2,1,0:T(2,128)(2,1)} %get-tuple-element.167) | copy-start | bytes 3538948
  956.0 14.3 copy-start.11
  956.0 14.3 copy-start.25
  1008.3 15.2 copy-start.1
  1032.0 13.8 copy-start.21
  1247.2 487.1 %all-reduce.11.cloned.1.call-start = ((), (), s32[]{:S(2)}) async-start(), calls=%async_computation.3 | async-start | bytes 37748736 | tf_op jit(solution)/shard_map/psum | solution.py:64
  1472.7 14.3 copy-start.12
  1472.7 14.3 copy-start.24
  1487.0 38.3 %copy-start.31 = (bf16[2,192,768]{2,1,0:T(8,128)(2,1)S(1)}, bf16[2,192,768]{2,1,0:T(8,128)(2,1)}, u32[]{:S(2)}) copy-start(bf16[2,192,768]{2,1,0:T(8,128)(2,1)} %param.31) | copy-start | bytes 1769476
  (16 other events, 138.9 us)
Sparse Core Ops, SparseCore 0:
  434.9 196.7 all-reduce.4
  730.7 193.9 all-reduce.6
  1247.3 193.9 all-reduce.8
  1540.2 193.9 all-reduce.10
where the time goes:
time: 1780 us; the launch traced here: 1770 us
  matrix products  771 us (43%)
  waiting for transfers between devices  570 us (32%)
  other arithmetic  307 us (17%)
  local copies, waits for them, and re-layouts  109 us (6%)
    psum x2, waiting for transfers between devices, shard_body(): trans_out = lax.psum(trans_part, 'tp').astype(jnp.float32)  306 us
    psum x2, waiting for transfers between devices, shard_body(): attn_out = lax.psum(attn_part, 'tp').astype(jnp.float32)  264 us
    dot_general x16, matrix products, attend_sample(): jnp.einsum('hqk,khc->qhc', attn_probs, value_one, preferred_element_type=...  210 us
    sub x16, matrix products, attend_sample(): attn_probs = jax.nn.softmax(logits, axis=-1).astype(jnp.bfloat16)  147 us
    unnamed x4, matrix products  142 us
    dot_general x4, matrix products, ada_norm(): jnp.einsum('rc,cgd->rgd', cond_in, weight, preferred_element_type=jnp.flo...  137 us
    reduce_sum x5, other arithmetic, layer_norm(): row_mean = jnp.mean(values_in, axis=-1, keepdims=True)  108 us
    dot_general x2, matrix products, shard_body(): jnp.einsum('rc,cgd->rgd', cond_flat, zero_w[layer_idx], preferred_element...  86.7 us
  transfers between devices with their start and end apart: 4, of which 4 were waited for; matrix products, arithmetic and copies ran while one was open for 12% of the time, Pallas kernels for 0%

commit v1 on v0

v1 whole, which is shorter than its diff:
```python
import functools
import math

import jax
import jax.numpy as jnp
import numpy as np
from jax import lax
from jax.experimental import pallas as pl
from jax.experimental.pallas import tpu as pltpu
from jax.sharding import PartitionSpec as P

LN_EPS = 1e-5
LOG2E = math.log2(math.e)
MASK_VALUE = 1e9
BLOCK = 128
QUERY_TILE = 256
KEY_TILE = 256
SCORE_TILE = 768
ROW_TILE = 512
HIDDEN_TILE = 512
CHUNK_SAMPLES = 2
LANES = 128
SUBLANES = 8
F32 = jnp.float32
BF16 = jnp.bfloat16


def dot(a, b):
    return jnp.dot(a, b, preferred_element_type=F32)


def dot_nt(a, b):
    return lax.dot_general(a, b, (((1,), (1,)), ((), ())), preferred_element_type=F32)


def dot_tn(a, b):
    return lax.dot_general(a, b, (((0,), (0,)), ((), ())), preferred_element_type=F32)


def sigmoid(x):
    return 0.5 * jnp.tanh(0.5 * x) + 0.5


def layer_norm(x):
    centered = x - jnp.mean(x, axis=-1, keepdims=True)
    variance = jnp.mean(centered * centered, axis=-1, keepdims=True)
    return centered * lax.rsqrt(variance + LN_EPS)


def mask_terms():
    left = np.float32(-MASK_VALUE * LOG2E)
    terms = []
    for _ in range(3):
        term = np.float32(np.asarray(left).astype(BF16))
        terms.append(float(term))
        left = np.float32(left - term)
    return terms


def cost(flops, bytes_accessed):
    return pl.CostEstimate(flops=int(flops), bytes_accessed=int(bytes_accessed), transcendentals=0)


def ada_norm(x_normed, cond_normed, scale, weight, bias):
    cond_in = (cond_normed * scale).astype(BF16)
    width = x_normed.shape[-1]
    parts = []
    for at in range(0, width, 256):
        gate = dot(cond_in, weight(0, at, 256))
        shift = dot(cond_in, weight(1, at, 256))
        parts.append((sigmoid(gate + bias[:, at:at + 256]) * x_normed[:, at:at + 256] + shift).astype(BF16))
    return jnp.concatenate(parts, axis=-1)


def write_projection(x1, w_ref, b_q_ref, mask_ref, q_ref, k_ref, v_ref, g_ref, head_dim, heads):
    used = heads * head_dim
    rows = x1.shape[0]
    made = dot_nt(w_ref[...], x1)
    query = (made[:used] + b_q_ref[...]).astype(BF16).astype(F32) * (LOG2E / math.sqrt(head_dim))
    high = query.astype(BF16)
    low = (query - high.astype(F32)).astype(BF16)
    row = lax.broadcasted_iota(jnp.int32, (LANES - used, rows), 0)
    ones = jnp.where(row < 3, 1.0, 0.0).astype(BF16)
    q_ref[0, :used] = high
    q_ref[0, used:LANES] = ones
    q_ref[0, LANES:LANES + used] = low
    q_ref[0, LANES + used:] = jnp.zeros_like(ones)
    keys = jnp.concatenate([made[used:2 * used], jnp.zeros((LANES - used, rows), F32)], axis=0).T
    k_ref[...] = (keys.astype(BF16).astype(F32) + mask_ref[...].astype(F32)).astype(BF16)
    v_ref[...] = made[2 * used:3 * used].astype(BF16).reshape(v_ref.shape)
    g_ref[...] = sigmoid(made[3 * used:]).reshape(g_ref.shape)


def first_kernel(act_ref, cond_ref, scale_ref, ada_w_ref, bias_ref, w_ref, b_q_ref, mask_ref, q_ref, k_ref, v_ref, g_ref, *, head_dim, heads):
    cond_normed = layer_norm(cond_ref[...].astype(F32))
    x_normed = layer_norm(act_ref[...].astype(F32))
    x1 = ada_norm(x_normed, cond_normed, scale_ref[...], lambda g, at, n: ada_w_ref[g, :, at:at + n], bias_ref[...])
    write_projection(x1, w_ref, b_q_ref, mask_ref, q_ref, k_ref, v_ref, g_ref, head_dim, heads)


def next_kernel(x1_ref, w_ref, b_q_ref, mask_ref, q_ref, k_ref, v_ref, g_ref, *, head_dim, heads):
    x1 = x1_ref[...].reshape(k_ref.shape[0], x1_ref.shape[-1])
    write_projection(x1, w_ref, b_q_ref, mask_ref, q_ref, k_ref, v_ref, g_ref, head_dim, heads)


def attend_kernel(bias_ref, q_ref, k_ref, v_ref, g_ref, out_ref, bias_t, scores_a, scores_b, send, send_sem, recv_sem, *, devices, head_dim, heads):
    tile, head = pl.program_id(0), pl.program_id(1)
    tiles = pl.num_programs(0)
    samples, tokens = k_ref.shape[0], k_ref.shape[1]
    blocks = tokens // BLOCK
    per_tile = QUERY_TILE // BLOCK
    slots = out_ref.shape[1]
    key_tiles = tokens // KEY_TILE
    me = lax.axis_index('tp')
    parity = lax.rem(tile, 2)
    row = lax.rem(lax.broadcasted_iota(jnp.int32, (2 * LANES, QUERY_TILE), 0), LANES)
    mine = ((row >= head * head_dim) & (row < (head + 1) * head_dim)) | (row >= heads * head_dim)

    def peer(step):
        return lax.rem(me + step, devices)

    def where_to(at_tile, sample, i):
        block = sample * blocks + at_tile * per_tile + i
        return lax.rem(block, devices), lax.div(block, devices)

    def local(at_tile, sample, i, slot):
        p = lax.rem(at_tile, 2)
        return pltpu.make_async_copy(send.at[p, sample, i], out_ref.at[me, slot], send_sem.at[p, sample, i])

    def remote(at_tile, sample, i, to, slot):
        p = lax.rem(at_tile, 2)
        return pltpu.make_async_remote_copy(
            src_ref=send.at[p, sample, i], dst_ref=out_ref.at[me, slot], send_sem=send_sem.at[p, sample, i],
            recv_sem=recv_sem.at[slot, me], device_id={'tp': to}, device_id_type=pl.DeviceIdType.MESH)

    def each(at_tile, local_do, remote_do):
        @pl.loop(0, samples)
        def _(sample):
            for i in range(per_tile):
                to, slot = where_to(at_tile, sample, i)

                @pl.when(to == me)
                def _():
                    local_do(local(at_tile, sample, i, slot))

                @pl.when(to != me)
                def _():
                    remote_do(remote(at_tile, sample, i, to, slot))

    @pl.when((tile == 0) & (head == 0))
    def _():
        barrier = pltpu.get_barrier_semaphore()
        for step in range(1, devices):
            pl.semaphore_signal(barrier, inc=1, device_id={'tp': peer(step)}, device_id_type=pl.DeviceIdType.MESH)
        pl.semaphore_wait(barrier, devices - 1)

    @pl.when((tile >= 2) & (head == 0))
    def _():
        each(tile - 2, lambda c: c.wait(), lambda c: c.wait_send())

    for at in range(0, tokens, KEY_TILE):
        bias_t[at:at + KEY_TILE, :] = bias_ref[:, at:at + KEY_TILE].astype(F32).T * LOG2E

    def score(sample, scores, kt, queries, top):
        at = kt * SCORE_TILE
        keys = k_ref[sample, at:at + SCORE_TILE, :]
        logits = dot(jnp.concatenate([keys, keys], axis=1), queries) + bias_t[at:at + SCORE_TILE, :]
        scores[at:at + SCORE_TILE, :] = logits
        part = jnp.max(logits.reshape(SCORE_TILE // SUBLANES, SUBLANES, QUERY_TILE), axis=0)
        return part if top is None else jnp.maximum(top, part)

    def queries_of(sample):
        return jnp.where(mine, q_ref[sample].astype(F32), 0.0).astype(BF16)

    def mix(sample, scores, kt, top, total, mixed):
        at = kt * KEY_TILE
        weights = jnp.exp2(scores[at:at + KEY_TILE, :] - top)
        part = jnp.sum(weights.reshape(KEY_TILE // SUBLANES, SUBLANES, QUERY_TILE), axis=0)
        value = dot(v_ref[sample, head, :, at:at + KEY_TILE], weights.astype(BF16))
        return (part, value) if total is None else (total + part, mixed + value)

    def finish(sample, total, mixed):
        norm = 1.0 / jnp.sum(total, axis=0, keepdims=True)
        done = (mixed * norm * g_ref[sample, head]).astype(BF16)
        for i in range(per_tile):
            send[parity, sample, i, head] = done[:, i * BLOCK:(i + 1) * BLOCK]

    def both(ahead, scores_ahead, sample, scores, top):
        queries = queries_of(ahead) if ahead is not None else None
        top = jnp.max(top, axis=0, keepdims=True) if sample is not None else None
        next_top = total = mixed = None
        for kt in range(key_tiles):
            if ahead is not None and kt % (SCORE_TILE // KEY_TILE) == 0:
                next_top = score(ahead, scores_ahead, kt // (SCORE_TILE // KEY_TILE), queries, next_top)
            if sample is not None:
                total, mixed = mix(sample, scores, kt, top, total, mixed)
        if sample is not None:
            finish(sample, total, mixed)
        return next_top

    top = both(0, scores_a, None, None, None)

    def pair(i, top):
        top = both(2 * i + 1, scores_b, 2 * i, scores_a, top)
        return both(2 * i + 2, scores_a, 2 * i + 1, scores_b, top)

    top = lax.fori_loop(0, samples // 2 - 1, pair, top)
    top = both(samples - 1, scores_b, samples - 2, scores_a, top)
    both(None, None, samples - 1, scores_b, top)

    @pl.when(head == heads - 1)
    def _():
        each(tile, lambda c: c.start(), lambda c: c.start())

    @pl.when((tile == tiles - 1) & (head == heads - 1))
    def _():
        each(tile - 1, lambda c: c.wait(), lambda c: c.wait_send())
        each(tile, lambda c: c.wait(), lambda c: c.wait_send())
        for step in range(1, devices):
            @pl.loop(0, slots)
            def _(slot):
                pltpu.make_async_remote_copy(
                    src_ref=send.at[0, 0, 0], dst_ref=out_ref.at[peer(step), slot], send_sem=send_sem.at[0, 0, 0],
                    recv_sem=recv_sem.at[slot, peer(step)], device_id={'tp': peer(step)},
                    device_id_type=pl.DeviceIdType.MESH).wait_recv()


def rows_kernel(me_ref, mixed_ref, act_ref, cond_ref, w_ref, zero_w_ref, ada_w_ref, next_w_ref, zero_b_ref, scale_ref, bias_ref, next_scale_ref, next_bias_ref, *rest, first_row, units, local_width):
    *outs, w_up1, w_up2, w_down, w_o, w_zero, w_ada, w_next, sem = rest
    devices = w_ref.shape[0]
    width = act_ref.shape[-1]
    last = len(outs) == 1

    def part(at, n):
        return w_ref.at[:, pl.ds(first_row + at, n)]

    copies = [
        pltpu.make_async_copy(zero_w_ref, w_zero, sem.at[0]),
        pltpu.make_async_copy(part(3 * units, local_width), w_o, sem.at[1]),
        pltpu.make_async_copy(ada_w_ref, w_ada, sem.at[2]),
        pltpu.make_async_copy(part(0, units), w_up1, sem.at[3]),
        pltpu.make_async_copy(part(units, units), w_up2, sem.at[4]),
        pltpu.make_async_copy(part(2 * units, units), w_down, sem.at[5]),
    ]
    if not last:
        copies.append(pltpu.make_async_copy(next_w_ref, w_next, sem.at[6]))
    for copy in copies:
        copy.start()
    slots = act_ref.shape[0]
    rows = slots * BLOCK
    cond = cond_ref[...].reshape(rows, cond_ref.shape[-1])
    cond_normed = layer_norm(cond.astype(F32))
    copies[0].wait()
    gates = [sigmoid(dot(cond, w_zero[g]) + zero_b_ref[g:g + 1]) for g in range(2)]
    copies[1].wait()
    weights_o = w_o[...].reshape(devices * local_width, width)
    attn = jnp.concatenate([dot_tn(mixed_ref[:, s].reshape(devices * local_width, BLOCK), weights_o) for s in range(slots)], axis=0)
    mid = (act_ref[...].reshape(rows, width).astype(F32) + gates[0] * attn.astype(BF16).astype(F32)).astype(BF16).astype(F32)
    copies[2].wait()
    normed = ada_norm(layer_norm(mid), cond_normed, scale_ref[...], lambda g, at, n: w_ada[g, :, at:at + n], bias_ref[...])
    copies[3].wait()
    copies[4].wait()
    up1 = w_up1[...].reshape(devices * units, width)
    up2 = w_up2[...].reshape(devices * units, width)
    hidden = []
    for at in range(0, devices * units, HIDDEN_TILE):
        u1 = dot_nt(normed, up1[at:at + HIDDEN_TILE])
        u2 = dot_nt(normed, up2[at:at + HIDDEN_TILE])
        hidden.append((u1 * sigmoid(u1) * u2).astype(BF16))
    copies[5].wait()
    moved = dot(jnp.concatenate(hidden, axis=-1), w_down[...].reshape(devices * units, width))
    act_new = (mid + gates[1] * moved.astype(BF16).astype(F32)).astype(BF16)
    outs[0][...] = act_new.reshape(outs[0].shape)
    if not last:
        copies[6].wait()
        x1 = ada_norm(layer_norm(act_new.astype(F32)), cond_normed, next_scale_ref[...], lambda g, at, n: w_next[g, :, at:at + n], next_bias_ref[...])
        outs[1][...] = x1.reshape(outs[1].shape)


def place_kernel(part_ref, *refs):
    refs[-1][0] = part_ref[:, 0]


def solution(mesh):
    devices = mesh.shape['tp']
    any_spec = pl.BlockSpec(memory_space=pl.ANY)

    def params(*semantics, limit=None, **more):
        return pltpu.CompilerParams(dimension_semantics=semantics or None, vmem_limit_bytes=limit, **more)

    def whole(shape):
        return pl.BlockSpec(shape, lambda *_: (0,) * len(shape), pipeline_mode=pl.Buffered(1))

    def shard_body(token_act, token_cond, pair_bias, token_mask, ada_scale, ada_w, ada_bias, zero_w, zero_b, w_qkvg, b_q, w_o, w_up, w_down):
        samples, tokens, width = token_act.shape
        cond_dim = token_cond.shape[-1]
        layers, heads = pair_bias.shape[:2]
        local_width = w_qkvg.shape[-1]
        head_dim = local_width // heads
        units = w_down.shape[1]
        chunk = CHUNK_SAMPLES
        chunks = samples // chunk
        slots = chunk * tokens // (devices * BLOCK)
        all_slots = slots * chunks
        me = lax.axis_index('tp').reshape(1).astype(jnp.int32)

        local_w = jnp.concatenate([part for l in range(layers) for part in (w_up[l, :, 0].T, w_up[l, :, 1].T, w_down[l], w_o[l])], axis=0)
        full_w = lax.all_gather(local_w, 'tp')
        ada_t = [[ada_w[l, j].transpose(1, 0, 2) for j in range(2)] for l in range(layers)]
        zero_t = [zero_w[l].transpose(1, 0, 2) for l in range(layers)]
        w_proj = [w_qkvg[l].reshape(width, 4 * local_width).T for l in range(layers)]
        b_q_col = [b_q[l].reshape(local_width, 1) for l in range(layers)]
        terms = jnp.zeros((LANES,), F32)
        for i, value in enumerate(mask_terms()):
            terms = terms.at[local_width + i].set(value)
        mask_rows = jnp.where(token_mask[:, None] == 0, terms[None, :], 0.0).astype(BF16)

        tiles = tokens // ROW_TILE
        proj_specs = [whole((4 * local_width, width)), whole((local_width, 1)),
                      pl.BlockSpec((ROW_TILE, LANES), lambda i: (lax.rem(i, tiles), 0))]

        def proj_outs(n):
            rows = pl.BlockSpec((ROW_TILE, LANES), lambda i: (i, 0))
            cols = pl.BlockSpec((1, heads, head_dim, ROW_TILE), lambda i: (lax.div(i, tiles), 0, 0, lax.rem(i, tiles)))
            shape_rows = jax.ShapeDtypeStruct((n * tokens, LANES), BF16)
            query = pl.BlockSpec((1, 2 * LANES, ROW_TILE), lambda i: (lax.div(i, tiles), 0, lax.rem(i, tiles)))
            return [query, rows, cols, cols], [jax.ShapeDtypeStruct((n, 2 * LANES, tokens), BF16), shape_rows,
                                               jax.ShapeDtypeStruct((n, heads, head_dim, tokens), BF16),
                                               jax.ShapeDtypeStruct((n, heads, head_dim, tokens), F32)]

        def proj_args(l):
            return w_proj[l], b_q_col[l], mask_rows

        def first():
            specs, shapes = proj_outs(samples)
            rows = samples * tokens
            return pl.pallas_call(
                functools.partial(first_kernel, head_dim=head_dim, heads=heads),
                grid=(rows // ROW_TILE,),
                in_specs=[pl.BlockSpec((ROW_TILE, width), lambda i: (i, 0)), pl.BlockSpec((ROW_TILE, cond_dim), lambda i: (i, 0)),
                          whole((1, cond_dim)), whole((2, cond_dim, width)), whole((1, width))] + proj_specs,
                out_specs=specs, out_shape=shapes, compiler_params=params('arbitrary'), name='first',
                cost_estimate=cost(2 * rows * (cond_dim * 2 * width + width * 4 * local_width), rows * width * 6),
            )(token_act.reshape(rows, width), token_cond.reshape(rows, cond_dim), ada_scale[0, 0:1], ada_t[0][0], ada_bias[0, 0:1], *proj_args(0))

        def following(x1, l):
            specs, shapes = proj_outs(chunk)
            rows = chunk * tokens
            per = ROW_TILE // BLOCK
            turns = devices // per
            return pl.pallas_call(
                functools.partial(next_kernel, head_dim=head_dim, heads=heads),
                grid=(rows // ROW_TILE,),
                in_specs=[pl.BlockSpec((per, 1, BLOCK, width), lambda i: (lax.rem(i, turns), lax.div(i, turns), 0, 0))] + proj_specs,
                out_specs=specs, out_shape=shapes, compiler_params=params('arbitrary'), name='following',
                cost_estimate=cost(2 * rows * width * 4 * local_width, rows * width * 6),
            )(x1, *proj_args(l))

        def attend(parts, n, l, collective_id):
            q, k, v, g = parts
            query = pl.BlockSpec((n, 2 * LANES, QUERY_TILE), lambda t, h: (0, 0, t))
            n_slots = n * tokens // (devices * BLOCK)
            shaped = (n, tokens, LANES)
            per_tile = QUERY_TILE // BLOCK
            return pl.pallas_call(
                functools.partial(attend_kernel, devices=devices, head_dim=head_dim, heads=heads),
                grid=(tokens // QUERY_TILE, heads),
                in_specs=[pl.BlockSpec((None, None, QUERY_TILE, tokens), lambda t, h: (l, h, t, 0)), query,
                          whole(shaped), whole((n, heads, head_dim, tokens)),
                          pl.BlockSpec((n, heads, head_dim, QUERY_TILE), lambda t, h: (0, 0, 0, t))],
                out_specs=any_spec,
                out_shape=jax.ShapeDtypeStruct((devices, n_slots, heads, head_dim, BLOCK), BF16),
                scratch_shapes=[pltpu.VMEM((tokens, QUERY_TILE), F32), pltpu.VMEM((tokens, QUERY_TILE), F32), pltpu.VMEM((tokens, QUERY_TILE), F32),
                                pltpu.VMEM((2, n, per_tile, heads, head_dim, BLOCK), BF16),
                                pltpu.SemaphoreType.DMA((2, n, per_tile)), pltpu.SemaphoreType.DMA((n_slots, devices))],
                compiler_params=params('arbitrary', 'arbitrary', collective_id=collective_id, has_side_effects=True), name='attend',
                cost_estimate=cost(4 * n * heads * tokens * tokens * 2 * LANES, heads * tokens * tokens * 2),
            )(pair_bias, q, k.reshape(shaped), v, g)

        def rows(mixed, act, l, c):
            last = l == layers - 1
            n_rows = slots * BLOCK
            nxt = 0 if last else l + 1
            own = pl.BlockSpec((slots, None, BLOCK, width), lambda i, me: (c, me[0], 0, 0))
            if l == 0:
                act, act_spec, mixed_at = token_act.reshape(all_slots, devices, BLOCK, width), own, c
            else:
                act_spec, mixed_at = pl.BlockSpec((slots, BLOCK, width), lambda i, me: (0, 0, 0)), 0
            small = lambda n: whole((1, n))
            out_spec = pl.BlockSpec((slots, BLOCK, width), lambda i, me: (0, 0, 0))
            out_shape = jax.ShapeDtypeStruct((slots, BLOCK, width), BF16)
            n_out = 1 if last else 2
            matrix = pltpu.VMEM((2, cond_dim, width), BF16)
            ups = pltpu.VMEM((devices, units, width), BF16)
            return pl.pallas_call(
                functools.partial(rows_kernel, first_row=l * (3 * units + local_width), units=units, local_width=local_width),
                grid_spec=pltpu.PrefetchScalarGridSpec(
                    num_scalar_prefetch=1, grid=(1,),
                    in_specs=[pl.BlockSpec((devices, slots, heads, head_dim, BLOCK), lambda i, me: (0, mixed_at, 0, 0, 0)), act_spec,
                              pl.BlockSpec((slots, None, BLOCK, cond_dim), lambda i, me: (c, me[0], 0, 0)),
                              any_spec, any_spec, any_spec, any_spec,
                              whole((2, width)), small(cond_dim), small(width), small(cond_dim), small(width)],
                    out_specs=[out_spec] * n_out,
                    scratch_shapes=[ups, ups, ups, pltpu.VMEM((devices, local_width, width), BF16), matrix, matrix, matrix, pltpu.SemaphoreType.DMA((7,))]),
                out_shape=[out_shape] * n_out, compiler_params=params('arbitrary'), name='rows',
                cost_estimate=cost(2 * n_rows * width * (width + 3 * devices * units + 6 * cond_dim), devices * (3 * units + local_width) * width * 2),
            )(me, mixed, act, token_cond.reshape(all_slots, devices, BLOCK, cond_dim), full_w, zero_t[l], ada_t[l][1], ada_t[nxt][0],
              zero_b[l], ada_scale[l, 1:2], ada_bias[l, 1:2], ada_scale[nxt, 0:1], ada_bias[nxt, 0:1])

        def place(out, part, c):
            first_one = out is None
            return pl.pallas_call(
                place_kernel, grid=(slots,),
                in_specs=[pl.BlockSpec((devices, 1, BLOCK, width), lambda i: (0, i, 0, 0))] + ([] if first_one else [any_spec]),
                out_specs=pl.BlockSpec((1, devices, BLOCK, width), lambda i: (c * slots + i, 0, 0, 0)),
                out_shape=jax.ShapeDtypeStruct((all_slots, devices, BLOCK, width), BF16),
                input_output_aliases={} if first_one else {1: 0},
                compiler_params=params('arbitrary'), name='place',
            )(*((part,) if first_one else (part, out)))

        mixed = attend(first(), samples, 0, 0)
        acts, x1s = [None] * chunks, [None] * chunks
        for c in range(chunks):
            acts[c], x1 = rows(mixed, None, 0, c)
            x1s[c] = lax.all_gather(x1, 'tp')
        out = None
        parts = []
        for l in range(1, layers):
            last = l == layers - 1
            for c in range(chunks):
                mixed = attend(following(x1s[c], l), chunk, l, 1 + (l - 1) * chunks + c)
                if last:
                    parts.append(lax.all_gather(rows(mixed, acts[c], l, c)[0], 'tp'))
                else:
                    acts[c], x1 = rows(mixed, acts[c], l, c)
                    x1s[c] = lax.all_gather(x1, 'tp')
        for c in range(chunks):
            out = place(out, parts[c], c)
        return out.reshape(samples, tokens, width)

    everywhere = P()
    in_specs = (P('dp', None, None), P('dp', None, None), P(None, 'tp', None, None), P(None), everywhere, everywhere, everywhere, everywhere, everywhere, P(None, None, None, 'tp'), P(None, 'tp'), P(None, 'tp', None), P(None, None, None, 'tp'), P(None, 'tp', None))
    return jax.shard_map(shard_body, mesh=mesh, in_specs=in_specs, out_specs=P('dp', None, None), check_vma=False)
```

time: 1780 us -> 451 us (0.25)
  matrix products: 771 us -> 0 us
  waiting for transfers between devices: 570 us -> 42.6 us
  Pallas kernels: 0 us -> 360 us
  other arithmetic: 307 us -> 1.73 us
  local copies, waits for them, and re-layouts: 109 us -> 22.8 us
    psum x4 -> x0, waiting for transfers between devices: 570 us -> none  [the longest x2 306 us: shard_body(): trans_out = lax.psum(trans_part, 'tp').astype(jnp.float32)]
    dot_general x26 -> x0, matrix products: 482 us -> none  [the longest x16 210 us: attend_sample(): jnp.einsum('hqk,khc->qhc', attn_probs, value_one, preferred_element_type=...]
    pallas_call x0 -> x22, Pallas kernels: none -> 360 us  [the longest x5 182 us: attend(): pl.pallas_call(functools.partial(attend_kernel, devices=devices, head_dim...]
    reduce_sum x10 -> x0, other arithmetic: 164 us -> none  [the longest x5 108 us: layer_norm(): row_mean = jnp.mean(values_in, axis=-1, keepdims=True)]
    sub x16 -> x0, matrix products: 147 us -> none  [attend_sample(): attn_probs = jax.nn.softmax(logits, axis=-1).astype(jnp.bfloat16)]
    unnamed x4 -> x0, matrix products: 142 us -> none
    convert_element_type x7 -> x1, other arithmetic: 111 us -> 1.03 us  [shard_body(): jnp.where(token_mask[:, None] == 0, terms[None, :], 0.0).astype(BF16)]
    unnamed x84 -> x27, local copies, waits for them, and re-layouts: 61.2 us -> 5.44 us
  transfers between devices with their start and end apart: 4 -> 9, of which waited for: 4 -> 2; matrix products, arithmetic and copies ran while one was open for 12% -> 4% of each run, Pallas kernels for 0% -> 78%
where the time goes in v1:
time: 451 us; the launch traced here: 443 us
  Pallas kernels  360 us (80%)
  waiting for transfers between devices  42.6 us (9%)
  local copies, waits for them, and re-layouts  22.8 us (5%)
  between operations  14 us (3%)
    pallas_call x5, Pallas kernels, attend(): pl.pallas_call(functools.partial(attend_kernel, devices=devices, head_dim...  182 us
    pallas_call x8, Pallas kernels, rows(): pl.pallas_call(functools.partial(rows_kernel, first_row=l * (3 * units +...  79.3 us
    pallas_call x1, Pallas kernels, first(): pl.pallas_call(functools.partial(first_kernel, head_dim=head_dim, heads=h...  47.4 us
    all_gather x4, waiting for transfers between devices, shard_body(): parts.append(lax.all_gather(rows(mixed, acts[c], l, c)[0], 'tp'))  42 us
    pallas_call x4, Pallas kernels, following(): pl.pallas_call(functools.partial(next_kernel, head_dim=head_dim, heads=he...  29.4 us
    pallas_call x4, Pallas kernels, place(): pl.pallas_call(place_kernel, grid=(slots,), in_specs=[pl.BlockSpec((devic...  21.6 us
  transfers between devices with their start and end apart: 9, of which 2 were waited for; matrix products, arithmetic and copies ran while one was open for 4% of the time, Pallas kernels for 78%

profile of v1, /device:TPU:113, one launch (start us, length us, event | category | flops | bytes accessed | tf_op | source)
XLA Modules:
  0.0 442.8 jit_solution(17945915029508135951)
XLA Ops:
  30.6 47.4 %first.1 = (bf16[8,256,1536]{2,1,0:T(8,128)(2,1)}, bf16[12288,128]{1,0:T(8,128)(2,1)}, bf16[8,2,48,1536]{3,2,1,0:T(8,128)(2,1)}, f32[8,2,48,1536]{3,2,1,0:T(8,128)}) custom-call(bf16[12288,768]{1,0:T(8,128)(2,1)} %bitcast.115, bf16[12288,384]{1,0:T(8,128)(2,1)} %bitcast.106, f32[1,384]{1,0:T(1,128)} %get-tuple-element.113.scale_ref.next_scale_ref, ...), custom_call_target="tpu_custom_call" | custom-call | flops 21743271936 | bytes 56623104 | tf_op jit(solution)/shard_map/first/pallas_call | solution.py:337
  78.0 68.7 %attend.5.mixed_ref = bf16[8,12,2,48,128]{4,3,2,1,0:T(8,128)(2,1)} custom-call(bf16[2,2,1536,1536]{3,2,1,0:T(8,128)(2,1)} %bias_ref.9, bf16[8,256,1536]{2,1,0:T(8,128)(2,1)} %get-tuple-element.69.q_ref, bf16[8,1536,128]{2,1,0:T(8,128)(2,1)} %bitcast.135, bf16[8,2,48,1536]{3,2,1,0:T(8,128)(2,1)} %get-tuple-element.71.v_ref, ...), custom_call_target="tpu_custom_call" | custom-call | flops 38654705664 | bytes 9437184 | tf_op jit(solution)/shard_map/attend/pallas_call | solution.py:365
  146.8 10.3 %rows.14 = (bf16[3,128,768]{2,1,0:T(8,128)(2,1)}, bf16[3,128,768]{2,1,0:T(8,128)(2,1)}) custom-call(s32[1]{0:T(128)} %bitcast.me_ref, bf16[8,12,2,48,128]{4,3,2,1,0:T(8,128)(2,1)} %attend.5.mixed_ref, bf16[12,8,128,768]{3,2,1,0:T(8,128)(2,1)} %bitcast.116, bf16[12,8,128,384]{3,2,1,0:T(8,128)(2,1)} %bitcast.107, bf16[8,1344,768]{2,1,0:T(8,128)(2,1)} %bitcast.98, ...), custom_call_target="tpu_custom_call" | custom-call | flops 4529848320 | bytes 8257536 | tf_op jit(solution)/shard_map/rows/pallas_call | solution.py:395
  157.3 10.3 %rows.12 = (bf16[3,128,768]{2,1,0:T(8,128)(2,1)}, bf16[3,128,768]{2,1,0:T(8,128)(2,1)}) custom-call(s32[1]{0:T(128)} %bitcast.me_ref, bf16[8,12,2,48,128]{4,3,2,1,0:T(8,128)(2,1)} %attend.5.mixed_ref, bf16[12,8,128,768]{3,2,1,0:T(8,128)(2,1)} %bitcast.117, bf16[12,8,128,384]{3,2,1,0:T(8,128)(2,1)} %bitcast.108, bf16[8,1344,768]{2,1,0:T(8,128)(2,1)} %bitcast.99, ...), custom_call_target="tpu_custom_call" | custom-call | flops 4529848320 | bytes 8257536 | tf_op jit(solution)/shard_map/rows/pallas_call | solution.py:395
  168.1 10.3 %rows.10 = (bf16[3,128,768]{2,1,0:T(8,128)(2,1)}, bf16[3,128,768]{2,1,0:T(8,128)(2,1)}) custom-call(s32[1]{0:T(128)} %bitcast.me_ref, bf16[8,12,2,48,128]{4,3,2,1,0:T(8,128)(2,1)} %attend.5.mixed_ref, bf16[12,8,128,768]{3,2,1,0:T(8,128)(2,1)} %bitcast.118, bf16[12,8,128,384]{3,2,1,0:T(8,128)(2,1)} %bitcast.109, bf16[8,1344,768]{2,1,0:T(8,128)(2,1)} %bitcast.100, ...), custom_call_target="tpu_custom_call" | custom-call | flops 4529848320 | bytes 8257536 | tf_op jit(solution)/shard_map/rows/pallas_call | solution.py:395
  178.6 10.3 %rows.8 = (bf16[3,128,768]{2,1,0:T(8,128)(2,1)}, bf16[3,128,768]{2,1,0:T(8,128)(2,1)}) custom-call(s32[1]{0:T(128)} %bitcast.me_ref, bf16[8,12,2,48,128]{4,3,2,1,0:T(8,128)(2,1)} %attend.5.mixed_ref, bf16[12,8,128,768]{3,2,1,0:T(8,128)(2,1)} %bitcast.119, bf16[12,8,128,384]{3,2,1,0:T(8,128)(2,1)} %bitcast.110, bf16[8,1344,768]{2,1,0:T(8,128)(2,1)} %bitcast.101, ...), custom_call_target="tpu_custom_call" | custom-call | flops 4529848320 | bytes 8257536 | tf_op jit(solution)/shard_map/rows/pallas_call | solution.py:395
  190.0 7.4 %following.7 = (bf16[2,256,1536]{2,1,0:T(8,128)(2,1)}, bf16[3072,128]{1,0:T(8,128)(2,1)}, bf16[2,2,48,1536]{3,2,1,0:T(8,128)(2,1)}, f32[2,2,48,1536]{3,2,1,0:T(8,128)}) custom-call(bf16[8,3,128,768]{3,2,1,0:T(8,128)(2,1)} %bitcast.134, bf16[384,768]{1,0:T(8,128)(2,1)} %bitcast.126, f32[96,1]{1,0:T(8,128)} %copy.34.b_q_ref, ...), custom_call_target="tpu_custom_call" | custom-call | flops 1811939328 | bytes 14155776 | tf_op jit(solution)/shard_map/following/pallas_call | solution.py:351
  197.4 27.7 %attend.9.mixed_ref = bf16[8,3,2,48,128]{4,3,2,1,0:T(8,128)(2,1)} custom-call(bf16[2,2,1536,1536]{3,2,1,0:T(8,128)(2,1)} %bias_ref.9, bf16[2,256,1536]{2,1,0:T(8,128)(2,1)} %get-tuple-element.92.q_ref, bf16[2,1536,128]{2,1,0:T(8,128)(2,1)} %bitcast.137, bf16[2,2,48,1536]{3,2,1,0:T(8,128)(2,1)} %get-tuple-element.94.v_ref, ...), custom_call_target="tpu_custom_call" | custom-call | flops 9663676416 | bytes 9437184 | tf_op jit(solution)/shard_map/attend/pallas_call | solution.py:365
  225.1 9.5 %rows.15 = bf16[3,128,768]{2,1,0:T(8,128)(2,1)} custom-call(s32[1]{0:T(128)} %bitcast.me_ref, bf16[8,3,2,48,128]{4,3,2,1,0:T(8,128)(2,1)} %attend.9.mixed_ref, bf16[3,128,768]{2,1,0:T(8,128)(2,1)} %get-tuple-element.96.act_ref, bf16[12,8,128,384]{3,2,1,0:T(8,128)(2,1)} %bitcast.111, bf16[8,1344,768]{2,1,0:T(8,128)(2,1)} %bitcast.102, ...), custom_call_target="tpu_custom_call" | custom-call | flops 4529848320 | bytes 8257536 | tf_op jit(solution)/shard_map/rows/pallas_call | solution.py:395
  235.0 7.4 %following.6 = (bf16[2,256,1536]{2,1,0:T(8,128)(2,1)}, bf16[3072,128]{1,0:T(8,128)(2,1)}, bf16[2,2,48,1536]{3,2,1,0:T(8,128)(2,1)}, f32[2,2,48,1536]{3,2,1,0:T(8,128)}) custom-call(bf16[8,3,128,768]{3,2,1,0:T(8,128)(2,1)} %bitcast.133, bf16[384,768]{1,0:T(8,128)(2,1)} %bitcast.127, f32[96,1]{1,0:T(8,128)} %copy.34.b_q_ref, ...), custom_call_target="tpu_custom_call" | custom-call | flops 1811939328 | bytes 14155776 | tf_op jit(solution)/shard_map/following/pallas_call | solution.py:351
  242.3 26.5 %attend.8.mixed_ref = bf16[8,3,2,48,128]{4,3,2,1,0:T(8,128)(2,1)} custom-call(bf16[2,2,1536,1536]{3,2,1,0:T(8,128)(2,1)} %bias_ref.9, bf16[2,256,1536]{2,1,0:T(8,128)(2,1)} %get-tuple-element.86.q_ref, bf16[2,1536,128]{2,1,0:T(8,128)(2,1)} %bitcast.138, bf16[2,2,48,1536]{3,2,1,0:T(8,128)(2,1)} %get-tuple-element.88.v_ref, ...), custom_call_target="tpu_custom_call" | custom-call | flops 9663676416 | bytes 9437184 | tf_op jit(solution)/shard_map/attend/pallas_call | solution.py:365
  268.8 9.5 %rows.13 = bf16[3,128,768]{2,1,0:T(8,128)(2,1)} custom-call(s32[1]{0:T(128)} %bitcast.me_ref, bf16[8,3,2,48,128]{4,3,2,1,0:T(8,128)(2,1)} %attend.8.mixed_ref, bf16[3,128,768]{2,1,0:T(8,128)(2,1)} %get-tuple-element.90.act_ref, bf16[12,8,128,384]{3,2,1,0:T(8,128)(2,1)} %bitcast.112, bf16[8,1344,768]{2,1,0:T(8,128)(2,1)} %bitcast.103, ...), custom_call_target="tpu_custom_call" | custom-call | flops 4529848320 | bytes 8257536 | tf_op jit(solution)/shard_map/rows/pallas_call | solution.py:395
  278.8 7.4 %following.5 = (bf16[2,256,1536]{2,1,0:T(8,128)(2,1)}, bf16[3072,128]{1,0:T(8,128)(2,1)}, bf16[2,2,48,1536]{3,2,1,0:T(8,128)(2,1)}, f32[2,2,48,1536]{3,2,1,0:T(8,128)}) custom-call(bf16[8,3,128,768]{3,2,1,0:T(8,128)(2,1)} %bitcast.132, bf16[384,768]{1,0:T(8,128)(2,1)} %bitcast.128, f32[96,1]{1,0:T(8,128)} %copy.34.b_q_ref, ...), custom_call_target="tpu_custom_call" | custom-call | flops 1811939328 | bytes 14155776 | tf_op jit(solution)/shard_map/following/pallas_call | solution.py:351
  286.1 30.5 %attend.7.mixed_ref = bf16[8,3,2,48,128]{4,3,2,1,0:T(8,128)(2,1)} custom-call(bf16[2,2,1536,1536]{3,2,1,0:T(8,128)(2,1)} %bias_ref.9, bf16[2,256,1536]{2,1,0:T(8,128)(2,1)} %get-tuple-element.80.q_ref, bf16[2,1536,128]{2,1,0:T(8,128)(2,1)} %bitcast.139, bf16[2,2,48,1536]{3,2,1,0:T(8,128)(2,1)} %get-tuple-element.82.v_ref, ...), custom_call_target="tpu_custom_call" | custom-call | flops 9663676416 | bytes 9437184 | tf_op jit(solution)/shard_map/attend/pallas_call | solution.py:365
  316.6 9.5 %rows.11 = bf16[3,128,768]{2,1,0:T(8,128)(2,1)} custom-call(s32[1]{0:T(128)} %bitcast.me_ref, bf16[8,3,2,48,128]{4,3,2,1,0:T(8,128)(2,1)} %attend.7.mixed_ref, bf16[3,128,768]{2,1,0:T(8,128)(2,1)} %get-tuple-element.84.act_ref, bf16[12,8,128,384]{3,2,1,0:T(8,128)(2,1)} %bitcast.113, bf16[8,1344,768]{2,1,0:T(8,128)(2,1)} %bitcast.104, ...), custom_call_target="tpu_custom_call" | custom-call | flops 4529848320 | bytes 8257536 | tf_op jit(solution)/shard_map/rows/pallas_call | solution.py:395
  326.6 7.4 %following.4 = (bf16[2,256,1536]{2,1,0:T(8,128)(2,1)}, bf16[3072,128]{1,0:T(8,128)(2,1)}, bf16[2,2,48,1536]{3,2,1,0:T(8,128)(2,1)}, f32[2,2,48,1536]{3,2,1,0:T(8,128)}) custom-call(bf16[8,3,128,768]{3,2,1,0:T(8,128)(2,1)} %bitcast.131, bf16[384,768]{1,0:T(8,128)(2,1)} %bitcast.129, f32[96,1]{1,0:T(8,128)} %copy.34.b_q_ref, ...), custom_call_target="tpu_custom_call" | custom-call | flops 1811939328 | bytes 14155776 | tf_op jit(solution)/shard_map/following/pallas_call | solution.py:351
  334.0 28.6 %attend.6.mixed_ref = bf16[8,3,2,48,128]{4,3,2,1,0:T(8,128)(2,1)} custom-call(bf16[2,2,1536,1536]{3,2,1,0:T(8,128)(2,1)} %bias_ref.9, bf16[2,256,1536]{2,1,0:T(8,128)(2,1)} %get-tuple-element.74.q_ref, bf16[2,1536,128]{2,1,0:T(8,128)(2,1)} %bitcast.136, bf16[2,2,48,1536]{3,2,1,0:T(8,128)(2,1)} %get-tuple-element.76.v_ref, ...), custom_call_target="tpu_custom_call" | custom-call | flops 9663676416 | bytes 9437184 | tf_op jit(solution)/shard_map/attend/pallas_call | solution.py:365
  362.5 9.5 %rows.9 = bf16[3,128,768]{2,1,0:T(8,128)(2,1)} custom-call(s32[1]{0:T(128)} %bitcast.me_ref, bf16[8,3,2,48,128]{4,3,2,1,0:T(8,128)(2,1)} %attend.6.mixed_ref, bf16[3,128,768]{2,1,0:T(8,128)(2,1)} %get-tuple-element.78.act_ref, bf16[12,8,128,384]{3,2,1,0:T(8,128)(2,1)} %bitcast.114, bf16[8,1344,768]{2,1,0:T(8,128)(2,1)} %bitcast.105, ...), custom_call_target="tpu_custom_call" | custom-call | flops 4529848320 | bytes 8257536 | tf_op jit(solution)/shard_map/rows/pallas_call | solution.py:395
  372.1 5.4 %place.4.refs_0_ = bf16[12,8,128,768]{3,2,1,0:T(8,128)(2,1)} custom-call(bf16[8,3,128,768]{3,2,1,0:T(8,128)(2,1)} %bitcast.122), custom_call_target="tpu_custom_call" | custom-call | tf_op jit(solution)/shard_map/place/pallas_call | solution.py:412
  377.5 5.4 %place.5.refs_0_ = bf16[12,8,128,768]{3,2,1,0:T(8,128)(2,1)} custom-call(bf16[8,3,128,768]{3,2,1,0:T(8,128)(2,1)} %bitcast.123, bf16[12,8,128,768]{3,2,1,0:T(8,128)(2,1)} %place.4.refs_0_), custom_call_target="tpu_custom_call", output_to_operand_aliasing={{}: (1, {})} | custom-call | tf_op jit(solution)/shard_map/place/pallas_call | solution.py:412
  382.9 15.9 %all-gather.27.cloned.1.call-done = bf16[24,128,768]{2,1,0:T(8,128)(2,1)} async-done(((bf16[3,128,768]{2,1,0:T(8,128)(2,1)}), bf16[24,128,768]{2,1,0:T(8,128)(2,1)}) %all-gather.27.cloned.1.call-update) | async-done | bytes 4718608 | tf_op jit(solution)/shard_map/all_gather | solution.py:433
  398.8 5.4 %place.6.refs_0_ = bf16[12,8,128,768]{3,2,1,0:T(8,128)(2,1)} custom-call(bf16[8,3,128,768]{3,2,1,0:T(8,128)(2,1)} %bitcast.124, bf16[12,8,128,768]{3,2,1,0:T(8,128)(2,1)} %place.5.refs_0_), custom_call_target="tpu_custom_call", output_to_operand_aliasing={{}: (1, {})} | custom-call | tf_op jit(solution)/shard_map/place/pallas_call | solution.py:412
  404.2 26.1 %all-gather.23.cloned.1.call-done = bf16[24,128,768]{2,1,0:T(8,128)(2,1)} async-done(((bf16[3,128,768]{2,1,0:T(8,128)(2,1)}), bf16[24,128,768]{2,1,0:T(8,128)(2,1)}) %all-gather.23.cloned.1.call-update) | async-done | bytes 4718608 | tf_op jit(solution)/shard_map/all_gather | solution.py:433
  430.3 5.4 %place.7 = bf16[12,8,128,768]{3,2,1,0:T(8,128)(2,1)} custom-call(bf16[8,3,128,768]{3,2,1,0:T(8,128)(2,1)} %bitcast.125, bf16[12,8,128,768]{3,2,1,0:T(8,128)(2,1)} %place.6.refs_0_), custom_call_target="tpu_custom_call", output_to_operand_aliasing={{}: (1, {})} | custom-call | tf_op jit(solution)/shard_map/place/pallas_call | solution.py:412
  (68 shorter events, 26.9 us)
Async XLA Ops:
  6.5 4.0 copy-start.2
  6.5 4.2 copy-start.4
  6.6 140.2 %all-gather.19.cloned.1.call-start = ((), (), s32[]{:S(2)}) async-start(), calls=%async_computation | async-start | bytes 18579456 | tf_op jit(solution)/shard_map/all_gather | solution.py:308
  6.6 4.1 copy-start.3
  10.6 1.6 copy-start.6
  10.6 4.4 copy-start.5
  10.8 1.3 copy-start
  12.1 7.3 %copy-start.1 = (bf16[2,384,2,768]{3,2,1,0:T(2,128)(2,1)S(1)}, bf16[2,384,2,768]{3,2,1,0:T(2,128)(2,1)}, u32[]{:S(2)}) copy-start(bf16[2,384,2,768]{3,2,1,0:T(2,128)(2,1)} %param.27) | copy-start | bytes 7077892
  12.2 177.9 %all-gather.33.cloned.1.call-start = ((), (), s32[]{:S(2)}) async-start(), calls=%async_computation.7 | async-start | bytes 5308416 | tf_op jit(solution)/shard_map/all_gather | solution.py:425
  17.0 5.9 %slice-start = ((s8[4718592]{0:T(1024)(128)(4,1)}), s8[4194304]{0:T(1024)(128)(4,1)S(1)}, s32[]{:S(2)}) async-start(s8[4718592]{0:T(1024)(128)(4,1)} %bitcast.120), calls=%async_computation.9 | async-start | bytes 8388608
  19.5 3.3 slice-start.1
  27.8 1.8 copy-start.7
  157.2 77.8 %all-gather.29.cloned.1.call-start = ((), (), s32[]{:S(2)}) async-start(), calls=%async_computation.5 | async-start | bytes 5308416 | tf_op jit(solution)/shard_map/all_gather | solution.py:425
  167.7 111.1 %all-gather.25.cloned.1.call-start = ((), (), s32[]{:S(2)}) async-start(), calls=%async_computation.3 | async-start | bytes 5308416 | tf_op jit(solution)/shard_map/all_gather | solution.py:425
  178.6 148.0 %all-gather.21.cloned.1.call-start = ((), (), s32[]{:S(2)}) async-start(), calls=%async_computation.1 | async-start | bytes 5308416 | tf_op jit(solution)/shard_map/all_gather | solution.py:425
  189.0 183.1 %all-gather.35.cloned.1.call-start = ((), (), s32[]{:S(2)}) async-start(), calls=%async_computation.8 | async-start | bytes 5308416 | tf_op jit(solution)/shard_map/all_gather | solution.py:433
  234.7 142.9 %all-gather.31.cloned.1.call-start = ((), (), s32[]{:S(2)}) async-start(), calls=%async_computation.6 | async-start | bytes 5308416 | tf_op jit(solution)/shard_map/all_gather | solution.py:433
  278.4 120.4 %all-gather.27.cloned.1.call-start = ((), (), s32[]{:S(2)}) async-start(), calls=%async_computation.4 | async-start | bytes 5308416 | tf_op jit(solution)/shard_map/all_gather | solution.py:433
  326.2 104.1 %all-gather.23.cloned.1.call-start = ((), (), s32[]{:S(2)}) async-start(), calls=%async_computation.2 | async-start | bytes 5308416 | tf_op jit(solution)/shard_map/all_gather | solution.py:433
Sparse Core Ops, SparseCore 0:
  12.3 83.3 all-gather.18
  157.3 32.5 all-gather.32
  191.5 36.2 all-gather.28
  229.1 31.5 all-gather.24
  262.2 29.8 all-gather.20
  293.5 34.8 all-gather.34
  330.0 37.2 all-gather.30
  368.9 29.9 all-gather.26
  400.4 29.8 all-gather.22
